TPU v7x, 128 devices: a whole 4x4x4 slice. The times are simulated.
128 devices in a mesh: seq: 8 (over z, core), head: 16 (over x, y).
Axes of the slice: x: 4, y: 4, z: 4, core: 2. Of those that a mesh axis runs over, the one named last changes fastest.
Arguments:
- lengths: int32 [16], replicated, may hold values from 128 to 8192, as said below
- page_owner: int32 [1536], replicated, may hold values from 0 to 16, as said below
- page_index: int32 [1536], replicated, may hold values from 0 to 127, as said below
- page_dest: int32 [1536], replicated, may hold values from 0 to 1535, as said below
- src_cache: bfloat16 [1536, 8, 64, 256], P(('seq', 'head')), may hold values from -8 to 8
- queries: bfloat16 [2, 16, 4096], replicated, may hold values from -8 to 8
- new_kv: bfloat16 [2, 16, 8, 256], replicated, may hold values from -6 to 6
- hidden_in: bfloat16 [2, 16, 4096], P(None, None, ('seq', 'head')), may hold values from -60 to 60
- out_weight: bfloat16 [4096, 4096], P(None, ('seq', 'head')), may hold values from -1.5 to 1.5
- norm_gain: bfloat16 [4096], P(('seq', 'head')), may hold values from 0.099609375 to 1.8984375
- router: bfloat16 [4096, 8], P(('seq', 'head')), may hold values from -0.09375 to 0.09375
- routes: int32 [2, 16, 2], replicated, may hold values from 0 to 7, all different within a row
- w_gate: bfloat16 [8, 4096, 8192], P('seq', None, 'head'), may hold values from -0.09375 to 0.09375
- w_up: bfloat16 [8, 4096, 8192], P('seq', None, 'head'), may hold values from -0.09375 to 0.09375
- w_down: bfloat16 [8, 8192, 4096], P('seq', 'head'), may hold values from -0.0625 to 0.0625
Outputs:
- page_pool: bfloat16 [16, 768, 64, 256], P('head', 'seq')
- mixed: bfloat16 [2, 16, 4096], P(None, None, ('seq', 'head'))
Inputs may be any that keep to these rules, and one draw needn't show every extreme that they name: Each length is at least 128; one equals 8192; the requests' pages, lengths[r] / 64 rounded up for request r, fit into the 1536 pages. `page_owner`: request r owns exactly lengths[r] / 64 rounded up source pages; the other pages carry 16. `page_index`: the pages of request r carry 0 to their count minus 1, each once; pages without request carry 0. `page_dest`: A permutation. Slot g belongs to destination group ((g % 768) // 96) * 2 + g // 768. Of the 12 pages that one device holds (pages i * 12 to (i + 1) * 12 - 1), at most 1 go to one group, and every draw has a device that sends exactly 1 to some group.
All inputs are finite; a program needn't handle non-finite values.
Results may differ from a plain program's by a relative error of at most 0.009.
Values may be sent and summed in bfloat16 or wider, within the bound.
A program may use at most 128 MiB of HBM per device.

v0:
```python
import jax
import jax.numpy as jnp
from jax import lax
from jax.sharding import Mesh
from jax.sharding import PartitionSpec as P

D = 4096
HQ = 32
KVH = 8
HD = 128
TOPK = 2
PAGE = 64
REQS = 16
SEQ = ("seq_0", "seq_1")
HEAD = ("head_0", "head_1")
SEQ_HEAD = ("seq_0", "seq_1", "head_0", "head_1")
NEG_FILL = -1e30
EPSILON = 1e-05
HIGHEST = lax.Precision.HIGHEST


def joined_all(array, axes, combine):
    for axis in axes:
        pieces = jax.tree.map(lambda part: lax.all_gather(part, axis), array)
        array = jax.tree.map(lambda part: part[0], pieces)
        for k in range(1, lax.axis_size(axis)):
            array = combine(array, jax.tree.map(lambda part: part[k], pieces))
    return array


def over_axes(array, axes):
    for axis in axes:
        array = lax.psum(array, axis)
    return array


def in_blocks(array, dim, peers):
    lengths = array.shape
    blocks = array.reshape(*lengths[:dim], peers, lengths[dim] // peers, *lengths[dim + 1 :])
    return jnp.moveaxis(blocks, dim, 0)


def cut_rows(length, count):
    unit = 8 if length >= 8 * count else 1
    return [length // unit * k // count * unit for k in range(1, count)]


def own_block(blocks, axes, sequence):
    lengths = [lax.axis_size(a) for a in axes]
    blocks = blocks.reshape(*lengths, *blocks.shape[1:])
    blocks = blocks.transpose(*sequence, *range(len(axes), blocks.ndim))
    blocks = blocks.reshape(-1, *blocks.shape[len(axes) :])
    for k in sequence:
        blocks = lax.psum_scatter(blocks, axes[k], scatter_dimension=0, tiled=True)
    return blocks[0]


def sum_all_axes_2(array, axes, dim):
    blocks = in_blocks(array, dim, lax.axis_size(axes))
    widest = max(range(1, max(2, blocks.ndim - 1)), key=lambda d: blocks.shape[d])
    count, gathered = (len(axes), [])
    for initial, share in enumerate(
        jnp.split(blocks, cut_rows(blocks.shape[widest], count), axis=widest)
    ):
        if share.size:
            sequence = [(initial + k) % count for k in range(count)]
            gathered.append(own_block(share, axes, sequence))
    return jnp.concatenate(gathered, axis=widest - 1)


def gate_mix(logits, picked):
    expert_ids = jnp.arange(logits.shape[1], dtype=jnp.int32)[None, :]
    first_hit = picked[:, 0:1] == expert_ids
    second_hit = picked[:, 1:2] == expert_ids
    first_logit = jnp.sum(jnp.where(first_hit, logits, 0.0), axis=1)
    second_logit = jnp.sum(jnp.where(second_hit, logits, 0.0), axis=1)
    leading = 1.0 / (1.0 + jnp.exp(second_logit - first_logit))
    trailing = 1.0 / (1.0 + jnp.exp(first_logit - second_logit))
    return jnp.where(first_hit, leading[:, None], 0.0) + jnp.where(
        second_hit, trailing[:, None], 0.0
    )


def combine(earlier, later):
    first_top, first_sum, first_acc = earlier
    second_top, second_sum, second_acc = later
    joint_top = jnp.maximum(first_top, second_top)
    first_factor = jnp.exp(first_top - joint_top)
    second_factor = jnp.exp(second_top - joint_top)
    return (
        joint_top,
        first_sum * first_factor + second_sum * second_factor,
        first_acc * first_factor[..., None] + second_acc * second_factor[..., None],
    )


def slot_plan(page_dest, pages_dev, slot_count, slots_dev, replicas, groups):
    part_index = page_dest // slot_count
    within = page_dest % slot_count
    target = within // slots_dev * replicas + part_index
    position = within % slots_dev
    per_device = target.reshape(-1, pages_dev)
    onehot = (per_device[:, :, None] == jnp.arange(groups, dtype=jnp.int32)[None, None, :]).astype(
        jnp.int32
    )
    before = jnp.cumsum(onehot, axis=1) - onehot
    ranking = jnp.sum(before * onehot, axis=2).reshape(-1)
    return (target, position, ranking)


def partial_attention(page_block, owners, page_pos, lengths, grouped, score_scale):
    head_dim = grouped.shape[-1]
    page_len = page_block.shape[2]
    requests = grouped.shape[1]
    clipped = jnp.minimum(owners, requests - 1)
    length_cap = jnp.take(lengths, clipped)
    offsets = page_pos[:, None] * page_len + jnp.arange(page_len, dtype=jnp.int32)[None, :]
    is_live = (owners < requests)[:, None] & (offsets < length_cap[:, None])
    live_mask = is_live[None, :, None, None, :]
    asked_rows = jnp.take(grouped, clipped, axis=1)
    scores = (
        jnp.einsum(
            "spkgd,pktd->spkgt",
            asked_rows,
            page_block[..., :head_dim],
            preferred_element_type=jnp.float32,
        )
        * score_scale
    )
    scores = jnp.where(live_mask, scores, NEG_FILL)
    members = owners[:, None] == jnp.arange(requests, dtype=jnp.int32)[None, :]
    page_top = jnp.max(scores, axis=4)
    row_top = jnp.max(
        jnp.where(members[None, :, :, None, None], page_top[:, :, None], NEG_FILL), axis=1
    )
    weights = jnp.where(
        live_mask, jnp.exp(scores - jnp.take(row_top, clipped, axis=1)[..., None]), 0.0
    )
    member_mask = members.astype(jnp.float32)
    totals = jnp.einsum("pr,spkg->srkg", member_mask, jnp.sum(weights, axis=4), precision=HIGHEST)
    page_out = jnp.einsum(
        "spkgt,pktd->spkgd",
        weights.astype(jnp.bfloat16),
        page_block[..., head_dim:],
        preferred_element_type=jnp.float32,
    )
    weighted = jnp.einsum("pr,spkgd->srkgd", member_mask, page_out, precision=HIGHEST)
    return (row_top, totals, weighted)


def body(
    lengths,
    page_owner,
    page_index,
    page_dest,
    src_cache,
    queries,
    new_kv,
    hidden_in,
    out_weight,
    norm_gain,
    router,
    routes,
    w_gate,
    w_up,
    w_down,
):
    seq_count = lax.axis_size(SEQ)
    head_count = lax.axis_size(HEAD)
    device_count = seq_count * head_count
    seq_pos = lax.axis_index(SEQ)
    head_pos = lax.axis_index(HEAD)
    pages_dev = src_cache.shape[0]
    page_total = page_dest.shape[0]
    replicas = head_count // KVH
    groups = seq_count * replicas
    slot_count = page_total // replicas
    slots_dev = pages_dev * KVH
    capacity = (slots_dev + device_count - 1) // device_count
    group_size = HQ // KVH
    step_count = queries.shape[0]
    row_count = step_count * REQS
    source = seq_pos * head_count + head_pos
    target, position, ranking = slot_plan(
        page_dest, pages_dev, slot_count, slots_dev, replicas, groups
    )
    local_target = lax.dynamic_slice_in_dim(target, source * pages_dev, pages_dev)
    local_rank = lax.dynamic_slice_in_dim(ranking, source * pages_dev, pages_dev)
    wanted = jnp.arange(groups * capacity, dtype=jnp.int32)
    matches = (local_target[None, :] == (wanted // capacity)[:, None]) & (
        local_rank[None, :] == (wanted % capacity)[:, None]
    )
    picked_page = jnp.sum(
        jnp.where(matches, jnp.arange(pages_dev, dtype=jnp.int32)[None, :], 0), axis=1
    )
    filled = jnp.any(matches, axis=1)
    packed = jnp.where(
        filled[:, None, None, None],
        jnp.take(src_cache, picked_page, axis=0),
        jnp.zeros((), jnp.bfloat16),
    )
    packed = packed.reshape(seq_count, replicas, capacity, KVH, PAGE, 2 * HD).transpose(
        0, 3, 1, 2, 4, 5
    )
    arrived = lax.all_to_all(
        packed.reshape(device_count, capacity, PAGE, 2 * HD),
        SEQ_HEAD,
        split_axis=0,
        concat_axis=0,
        tiled=True,
    )
    arrived = arrived.reshape(device_count * capacity, PAGE, 2 * HD)
    my_group = seq_pos * replicas + head_pos % replicas
    slot_ids = jnp.arange(slots_dev, dtype=jnp.int32)
    holders = (target[None, :] == my_group) & (position[None, :] == slot_ids[:, None])
    flat_index = jnp.arange(page_total, dtype=jnp.int32) // pages_dev * capacity + ranking
    chosen = jnp.sum(jnp.where(holders, flat_index[None, :], 0), axis=1)
    page_pool = jnp.take(arrived, chosen, axis=0)
    grouped = queries.reshape(step_count, REQS, KVH, group_size, HD)
    score_scale = HD ** (-0.5)
    kv_head = head_pos // replicas
    owners = jnp.sum(jnp.where(holders, page_owner[None, :], 0), axis=1)
    places = jnp.sum(jnp.where(holders, page_index[None, :], 0), axis=1)
    own_queries = lax.dynamic_slice_in_dim(grouped, kv_head, 1, axis=2)
    row_top, totals, weighted = partial_attention(
        page_pool[:, None], owners, places, lengths, own_queries, score_scale
    )
    owned_head = (jnp.arange(KVH, dtype=jnp.int32) == kv_head)[None, None, :, None]
    row_top = jnp.where(owned_head, row_top, NEG_FILL)
    totals = jnp.where(owned_head, totals, 0.0)
    weighted = jnp.where(owned_head[..., None], weighted, 0.0)
    row_top, totals, weighted = joined_all(
        (
            row_top.reshape(step_count, REQS, HQ),
            totals.reshape(step_count, REQS, HQ),
            weighted.reshape(step_count, REQS, HQ, HD),
        ),
        SEQ_HEAD,
        combine,
    )
    fresh_scores = (
        jnp.einsum(
            "srkgd,urkd->srkgu", grouped, new_kv[..., :HD], preferred_element_type=jnp.float32
        )
        * score_scale
    )
    causal = (jnp.arange(step_count)[:, None] >= jnp.arange(step_count)[None, :])[:, None, None, :]
    fresh_scores = jnp.where(
        causal, fresh_scores.reshape(step_count, REQS, HQ, step_count), NEG_FILL
    )
    joint_top = jnp.maximum(row_top, jnp.max(fresh_scores, axis=3))
    factor = jnp.exp(row_top - joint_top)
    fresh_weights = jnp.where(causal, jnp.exp(fresh_scores - joint_top[..., None]), 0.0)
    totals = totals * factor + jnp.sum(fresh_weights, axis=3)
    fresh_rounded = fresh_weights.reshape(step_count, REQS, KVH, group_size, step_count).astype(
        jnp.bfloat16
    )
    fresh_out = jnp.einsum(
        "srkgu,urkd->srkgd", fresh_rounded, new_kv[..., HD:], preferred_element_type=jnp.float32
    )
    weighted = weighted * factor[..., None] + fresh_out.reshape(step_count, REQS, HQ, HD)
    attended = (weighted / totals[..., None]).reshape(row_count, HQ * HD).astype(jnp.bfloat16)
    attn_out = jnp.dot(attended, out_weight, preferred_element_type=jnp.float32)
    middle = hidden_in.reshape(row_count, -1).astype(jnp.float32) + attn_out
    gain_row = norm_gain.astype(jnp.float32)[None, :]
    squares, routed = (
        over_axes(jnp.sum(middle * middle, axis=1), SEQ_HEAD),
        over_axes(
            jnp.dot(middle * gain_row, router.astype(jnp.float32), precision=HIGHEST), SEQ_HEAD
        ),
    )
    inverse_rms = lax.rsqrt(squares / D + EPSILON)
    logits = routed * inverse_rms[:, None]
    normed = (middle * inverse_rms[:, None] * gain_row).astype(jnp.bfloat16)
    features = lax.all_gather(normed, SEQ_HEAD, axis=1, tiled=True)
    mixture = gate_mix(logits, routes.reshape(row_count, TOPK))
    local_experts = w_gate.shape[0]
    local_mix = lax.dynamic_slice_in_dim(mixture, seq_pos * local_experts, local_experts, axis=1)
    gate_act = jnp.einsum("rd,edf->erf", features, w_gate, preferred_element_type=jnp.float32)
    upward = jnp.einsum("rd,edf->erf", features, w_up, preferred_element_type=jnp.float32)
    inner_act = (jax.nn.silu(gate_act) * upward).astype(jnp.bfloat16)
    produced = jnp.einsum("erf,efd->erd", inner_act, w_down, preferred_element_type=jnp.float32)
    moe_out = sum_all_axes_2(jnp.sum(local_mix.T[:, :, None] * produced, axis=0).T, SEQ_HEAD, 0)
    mixed = (middle + moe_out.T).astype(jnp.bfloat16).reshape(step_count, REQS, -1)
    return (page_pool[None], mixed)


def solution(mesh):
    split = Mesh(mesh.devices.reshape(4, 2, 4, 4), ("seq_0", "seq_1", "head_0", "head_1"))
    in_specs = (
        P(),
        P(),
        P(),
        P(),
        P(SEQ_HEAD, None, None, None),
        P(),
        P(),
        P(None, None, SEQ_HEAD),
        P(None, SEQ_HEAD),
        P(SEQ_HEAD),
        P(SEQ_HEAD, None),
        P(),
        P(SEQ, None, HEAD),
        P(SEQ, None, HEAD),
        P(SEQ, HEAD, None),
    )
    out_specs = (P(HEAD, SEQ, None, None), P(None, None, SEQ_HEAD))
    return jax.shard_map(body, mesh=split, in_specs=in_specs, out_specs=out_specs, check_vma=False)
```

profile of v0, /device:TPU:0, one launch (start us, length us, event | category | flops | bytes accessed | tf_op | source)
XLA Modules:
  0.0 609.9 jit_solution(12945465828086669318)
XLA Ops:
  9.1 2.7 gather_fusion
  11.9 2.7 select_bitcast_fusion
  14.6 2.3 copy.230
  16.9 11.7 %all-to-all-start = ((bf16[128,1,64,256]{3,2,1,0:T(8,128)(2,1)}), bf16[128,1,64,256]{3,2,1,0:T(8,128)(2,1)}, u32[]{:S(2)}, u32[]{:S(2)}) async-start(bf16[128,1,64,256]{3,2,1,0:T(8,128)(2,1)} %bitcast.483), calls=%async_computation | async-start | bytes 8388608 | tf_op jit(solution)/shard_map/all_to_all | solution.py:205
  31.8 9.8 %fusion.130 = (s32[96]{0:T(128)S(1)}, s32[96]{0:T(128)S(1)}) fusion(s32[]{:T(128)} %bitcast.17, s32[]{:T(128)} %bitcast.18, s32[]{:T(128)} %bitcast.19, s32[]{:T(128)} %bitcast.20, s32[]{:T(128)} %bitcast.21, s32[]{:T(128)} %bitcast.22, s32[]{:T(128)} %bitcast.23, s32[]{:T(128)} %bitcast.24, s32[]{:T(128)} %bitcast.25, s32[]{:T(128)} %bitcast.26, ...), kind=kLoop, calls=%fused_computation.273 | loop fusion | flops 4032 | bytes 1600 | tf_op jit(solution)/shard_map/jit(_take)/select_n | solution.py:116
  41.7 38.0 %all-to-all-done = bf16[128,1,64,256]{3,2,1,0:T(8,128)(2,1)} async-done(((bf16[128,1,64,256]{3,2,1,0:T(8,128)(2,1)}), bf16[128,1,64,256]{3,2,1,0:T(8,128)(2,1)}, u32[]{:S(2)}, u32[]{:S(2)}) %all-to-all-start) | async-done | bytes 4194336 | tf_op jit(solution)/shard_map/all_to_all | solution.py:205
  79.7 3.0 gather_fusion.1
  88.4 2.0 fusion.8
  92.8 12.2 %all_gather.49 = f32[4,2,16,32]{3,2,1,0:T(8,128)S(1)} all-gather(f32[1,2,16,32]{3,2,1,0:T(8,128)S(1)} %copy.236), channel_id=1, replica_groups=mesh['seq_0'=4,'seq_1'=2,'head_0'=4,'head_1'=4] {'seq_0'}, dimensions={0}, use_global_device_ids=true | all-gather | bytes 20480 | tf_op jit(solution)/shard_map/all_gather | solution.py:24
  105.0 14.8 %all-gather.5.cloned.1.call-done = f32[4,2,16,32,128]{4,3,2,1,0:T(8,128)} async-done(((f32[1,2,16,32,128]{4,3,2,1,0:T(8,128)}), f32[4,2,16,32,128]{4,3,2,1,0:T(8,128)}) %all-gather.5.cloned.1.call-update) | async-done | bytes 2097168 | tf_op jit(solution)/shard_map/all_gather | solution.py:24
  119.8 2.9 fusion.45
  122.8 12.0 %all_gather.56 = f32[4,2,16,32]{3,2,1,0:T(8,128)S(1)} all-gather(f32[1,2,16,32]{3,2,1,0:T(8,128)S(1)} %copy.255), channel_id=1, replica_groups=mesh['seq_0'=4,'seq_1'=2,'head_0'=4,'head_1'=4] {'seq_0'}, dimensions={0}, use_global_device_ids=true | all-gather | bytes 20480 | tf_op jit(solution)/shard_map/all_gather | solution.py:24
  136.7 2.3 fusion.44
  141.0 12.1 %all_gather.53 = f32[4,2,16,32]{3,2,1,0:T(8,128)S(1)} all-gather(f32[1,2,16,32]{3,2,1,0:T(8,128)S(1)} %get-tuple-element.32), channel_id=1, replica_groups=mesh['seq_0'=4,'seq_1'=2,'head_0'=4,'head_1'=4] {'head_0'}, dimensions={0}, use_global_device_ids=true | all-gather | bytes 20480 | tf_op jit(solution)/shard_map/all_gather | solution.py:24
  153.1 16.3 %all-gather.9.cloned.1.call-done = f32[4,2,16,32,128]{4,3,2,1,0:T(8,128)} async-done(((f32[1,2,16,32,128]{4,3,2,1,0:T(8,128)}), f32[4,2,16,32,128]{4,3,2,1,0:T(8,128)}) %all-gather.9.cloned.1.call-update) | async-done | bytes 2097168 | tf_op jit(solution)/shard_map/all_gather | solution.py:24
  169.5 2.9 fusion.39
  172.5 2.4 fusion.152
  175.3 11.9 %all_gather.58 = f32[4,2,16,32]{3,2,1,0:T(8,128)S(1)} all-gather(f32[1,2,16,32]{3,2,1,0:T(8,128)S(1)} %get-tuple-element.31), channel_id=1, replica_groups=mesh['seq_0'=4,'seq_1'=2,'head_0'=4,'head_1'=4] {'head_0'}, dimensions={0}, use_global_device_ids=true | all-gather | bytes 20480 | tf_op jit(solution)/shard_map/all_gather | solution.py:24
  187.1 13.0 %all_gather.55 = f32[4,2,16,32]{3,2,1,0:T(8,128)S(1)} all-gather(f32[1,2,16,32]{3,2,1,0:T(8,128)S(1)} %get-tuple-element.30), channel_id=1, replica_groups=mesh['seq_0'=4,'seq_1'=2,'head_0'=4,'head_1'=4] {'head_1'}, dimensions={0}, use_global_device_ids=true | all-gather | bytes 20480 | tf_op jit(solution)/shard_map/all_gather | solution.py:24
  201.5 11.9 %all_gather.59 = f32[4,2,16,32]{3,2,1,0:T(8,128)S(1)} all-gather(f32[1,2,16,32]{3,2,1,0:T(8,128)S(1)} %get-tuple-element.29), channel_id=1, replica_groups=mesh['seq_0'=4,'seq_1'=2,'head_0'=4,'head_1'=4] {'head_1'}, dimensions={0}, use_global_device_ids=true | all-gather | bytes 20480 | tf_op jit(solution)/shard_map/all_gather | solution.py:24
  218.5 3.6 multiply_reduce_fusion
  222.3 10.7 %all-reduce.6 = (f32[32]{0:T(128)S(1)}, f32[32,8]{0,1:T(8,128)S(1)}) all-reduce(f32[32]{0:T(128)S(1)} %get-tuple-element.95, f32[32,8]{0,1:T(8,128)S(1)} %fusion.112), channel_id=1, replica_groups=mesh['seq_0'=4,'seq_1'=2,'head_0'=4,'head_1'=4] {'seq_0'}, use_global_device_ids=true, to_apply=%region_17.18 | all-reduce | flops 288 | bytes 2304 | tf_op jit(solution)/shard_map/psum | solution.py:33
  233.0 2.5 all-reduce.7
  235.5 8.7 %all-reduce.5 = (f32[32]{0:T(128)S(1)}, f32[32,8]{0,1:T(8,128)S(1)}) all-reduce(f32[32]{0:T(128)S(1)} %get-tuple-element.15, f32[32,8]{0,1:T(8,128)S(1)} %get-tuple-element.16), channel_id=1, replica_groups=mesh['seq_0'=4,'seq_1'=2,'head_0'=4,'head_1'=4] {'head_0'}, use_global_device_ids=true, to_apply=%region_19.20 | all-reduce | flops 288 | bytes 2304 | tf_op jit(solution)/shard_map/psum | solution.py:33
  244.3 10.3 %all-reduce.4 = (f32[32]{0:T(128)S(1)}, f32[32,8]{0,1:T(8,128)S(1)}) all-reduce(f32[32]{0:T(128)S(1)} %get-tuple-element.11, f32[32,8]{0,1:T(8,128)S(1)} %get-tuple-element.12), channel_id=1, replica_groups=mesh['seq_0'=4,'seq_1'=2,'head_0'=4,'head_1'=4] {'head_1'}, use_global_device_ids=true, to_apply=%region_20.21 | all-reduce | flops 288 | bytes 2304 | tf_op jit(solution)/shard_map/psum | solution.py:33
  254.6 60.0 %all_gather.60 = bf16[32,4096]{0,1:T(8,128)(2,1)S(1)} all-gather(bf16[32,32]{0,1:T(8,128)(2,1)S(1)} %multiply_convert_fusion), channel_id=1, replica_groups=mesh['seq_0'=4,'seq_1'=2,'head_0'=4,'head_1'=4] {'seq_0','seq_1','head_0..., dimensions={1}, use_global_device_ids=true | all-gather | bytes 264192 | tf_op jit(solution)/shard_map/all_gather | solution.py:275
  314.7 3.0 fusion.14
  317.7 5.1 fusion
  323.5 4.9 fusion.144
  328.5 2.9 copy.267
  331.5 3.1 copy.266
  335.4 15.0 %reduce-scatter.31.cloned.1.call-done = f32[32,8,32]{2,1,0:T(8,128)} async-done(((f32[128,8,32]{2,1,0:T(8,128)}), f32[32,8,32]{2,1,0:T(8,128)}) %reduce-scatter.31.cloned.1.call-update) | async-done | bytes 32784 | tf_op jit(solution)/shard_map/reduce_scatter | solution.py:54
  350.4 23.5 %reduce-scatter.25.cloned.1.call-done = f32[32,8,32]{2,1,0:T(8,128)} async-done(((f32[128,8,32]{2,1,0:T(8,128)}), f32[32,8,32]{2,1,0:T(8,128)}) %reduce-scatter.25.cloned.1.call-update) | async-done | bytes 32784 | tf_op jit(solution)/shard_map/reduce_scatter | solution.py:54
  374.0 32.0 %reduce-scatter.13.cloned.1.call-done = f32[32,8,32]{1,0,2:T(8,128)} async-done(((f32[128,8,32]{1,0,2:T(8,128)}), f32[32,8,32]{1,0,2:T(8,128)}) %reduce-scatter.13.cloned.1.call-update) | async-done | bytes 32784 | tf_op jit(solution)/shard_map/reduce_scatter | solution.py:54
  408.2 20.8 %reduce-scatter.33.cloned.1.call-done = f32[8,8,32]{2,1,0:T(8,128)} async-done(((f32[32,8,32]{2,1,0:T(8,128)}), f32[8,8,32]{2,1,0:T(8,128)}) %reduce-scatter.33.cloned.1.call-update) | async-done | bytes 8208 | tf_op jit(solution)/shard_map/reduce_scatter | solution.py:54
  429.0 22.5 %reduce-scatter.27.cloned.1.call-done = f32[8,8,32]{2,1,0:T(8,128)} async-done(((f32[32,8,32]{2,1,0:T(8,128)}), f32[8,8,32]{2,1,0:T(8,128)}) %reduce-scatter.27.cloned.1.call-update) | async-done | bytes 8208 | tf_op jit(solution)/shard_map/reduce_scatter | solution.py:54
  454.1 9.8 %reduce-scatter.15.cloned.1.call-done = f32[16,8,32]{1,0,2:T(8,128)} async-done(((f32[32,8,32]{1,0,2:T(8,128)}), f32[16,8,32]{1,0,2:T(8,128)}) %reduce-scatter.15.cloned.1.call-update) | async-done | bytes 16400 | tf_op jit(solution)/shard_map/reduce_scatter | solution.py:54
  465.7 4.1 bitcast_select_fusion.1
  469.8 8.4 %reduce-scatter.19.cloned.1.call-done = f32[64,8,32]{2,1,0:T(8,128)} async-done(((f32[128,8,32]{2,1,0:T(8,128)}), f32[64,8,32]{2,1,0:T(8,128)}) %reduce-scatter.19.cloned.1.call-update) | async-done | bytes 65552 | tf_op jit(solution)/shard_map/reduce_scatter | solution.py:54
  478.3 13.6 %reduce-scatter.35.cloned.1.call-done = f32[4,8,32]{2,1,0:T(8,128)} async-done(((f32[8,8,32]{2,1,0:T(8,128)}), f32[4,8,32]{2,1,0:T(8,128)}) %reduce-scatter.35.cloned.1.call-update) | async-done | bytes 4112 | tf_op jit(solution)/shard_map/reduce_scatter | solution.py:54
  491.9 17.7 %all-reduce.3 = f32[4,8,32]{2,1,0:T(8,128)S(1)} all-reduce(f32[4,8,32]{2,1,0:T(8,128)} %reduce-scatter.35.cloned.1.call-done), channel_id=17, replica_groups=mesh['seq_0'=4,'seq_1'=2,'head_0'=4,'head_1'=4] {'head_0'}, use_global_device_ids=true, to_apply=%region_38.39.clone | all-reduce | flops 1024 | bytes 8192
  510.2 6.3 %reduce-scatter.29.cloned.1.call-done = f32[2,8,32]{2,1,0:T(8,128)} async-done(((f32[8,8,32]{2,1,0:T(8,128)}), f32[2,8,32]{2,1,0:T(8,128)}) %reduce-scatter.29.cloned.1.call-update) | async-done | bytes 2064 | tf_op jit(solution)/shard_map/reduce_scatter | solution.py:54
  516.5 2.6 all-reduce.2
  519.8 19.1 %reduce-scatter.17.cloned.1.call-done = f32[4,8,32]{2,1,0:T(8,128)} async-done(((f32[16,8,32]{2,1,0:T(8,128)}), f32[4,8,32]{2,1,0:T(8,128)}) %reduce-scatter.17.cloned.1.call-update) | async-done | bytes 4112 | tf_op jit(solution)/shard_map/reduce_scatter | solution.py:54
  538.8 17.5 %all-reduce = f32[4,8,32]{2,1,0:T(8,128)S(1)} all-reduce(f32[4,8,32]{2,1,0:T(8,128)} %reduce-scatter.17.cloned.1.call-done), channel_id=5, replica_groups=mesh['seq_0'=4,'seq_1'=2,'head_0'=4,'head_1'=4] {'head_1'}, use_global_device_ids=true, to_apply=%region_26.27.clone | all-reduce | flops 1024 | bytes 8192
  556.4 5.3 reduce-scatter.21.cloned.1.call-done
  562.3 22.0 %reduce-scatter.23.cloned.1.call-done = f32[4,8,32]{2,1,0:T(8,128)} async-done(((f32[16,8,32]{2,1,0:T(8,128)}), f32[4,8,32]{2,1,0:T(8,128)}) %reduce-scatter.23.cloned.1.call-update) | async-done | bytes 4112 | tf_op jit(solution)/shard_map/reduce_scatter | solution.py:54
  584.3 17.7 %all-reduce.1 = f32[4,8,32]{2,1,0:T(8,128)S(1)} all-reduce(f32[4,8,32]{2,1,0:T(8,128)} %reduce-scatter.23.cloned.1.call-done), channel_id=9, replica_groups=mesh['seq_0'=4,'seq_1'=2,'head_0'=4,'head_1'=4] {'seq_0'}, use_global_device_ids=true, to_apply=%region_30.31.clone | all-reduce | flops 1024 | bytes 8192
  (201 shorter events, 35.8 us)
Async XLA Ops:
  7.2 2.0 copy-start
  16.9 11.8 %copy-start.6 = (bf16[2,16,4096]{2,1,0:T(8,128)(2,1)S(1)}, bf16[2,16,4096]{2,1,0:T(8,128)(2,1)}, u32[]{:S(2)}) copy-start(bf16[2,16,4096]{2,1,0:T(8,128)(2,1)} %param.20) | copy-start | bytes 786436
  16.9 12.2 %copy-start.10 = (s32[1536]{0:T(1024)S(1)}, s32[1536]{0:T(1024)}, u32[]{:S(2)}) copy-start(s32[1536]{0:T(1024)} %param.18) | copy-start | bytes 18436
  16.9 12.2 %copy-start.12 = (s32[1536]{0:T(1024)S(1)}, s32[1536]{0:T(1024)}, u32[]{:S(2)}) copy-start(s32[1536]{0:T(1024)} %param.17) | copy-start | bytes 18436
  16.9 12.2 %copy-start.13 = (s32[1536]{0:T(1024)S(1)}, s32[1536]{0:T(1024)}, u32[]{:S(2)}) copy-start(s32[1536]{0:T(1024)} %param.16) | copy-start | bytes 18436
  16.9 14.2 %copy-start.9 = (s32[16]{0:T(128)S(1)}, s32[16]{0:T(128)}, u32[]{:S(2)}) copy-start(s32[16]{0:T(128)} %param.15) | copy-start | bytes 196
  16.9 62.8 %all-to-all-start = ((bf16[128,1,64,256]{3,2,1,0:T(8,128)(2,1)}), bf16[128,1,64,256]{3,2,1,0:T(8,128)(2,1)}, u32[]{:S(2)}, u32[]{:S(2)}) async-start(bf16[128,1,64,256]{3,2,1,0:T(8,128)(2,1)} %bitcast.483), calls=%async_computation | async-start | bytes 8388608 | tf_op jit(solution)/shard_map/all_to_all | solution.py:205
  28.6 91.2 %all-gather.5.cloned.1.call-start = ((), (), s32[]{:S(2)}) async-start(), calls=%async_computation.13 | async-start | bytes 2621440 | tf_op jit(solution)/shard_map/all_gather | solution.py:24
  82.7 1.7 copy-start.2
  82.7 3.3 copy-start.7
  84.3 1.7 copy-start.4
  91.7 45.0 %all-gather.7.cloned.1.call-start = ((), (), s32[]{:S(2)}) async-start(), calls=%async_computation.14 | async-start | bytes 1572864 | tf_op jit(solution)/shard_map/all_gather | solution.py:24
  122.7 49.7 %copy-start.11 = (bf16[2,16,32]{2,1,0:T(8,128)(2,1)S(1)}, bf16[2,16,32]{2,1,0:T(8,128)(2,1)}, u32[]{:S(2)}) copy-start(bf16[2,16,32]{2,1,0:T(8,128)(2,1)} %param.22) | copy-start | bytes 6148
  122.7 46.8 %all-gather.9.cloned.1.call-start = ((), (), s32[]{:S(2)}) async-start(), calls=%async_computation.15 | async-start | bytes 2621440 | tf_op jit(solution)/shard_map/all_gather | solution.py:24
  122.8 49.7 %copy-start.8 = (bf16[2,16,8,256]{3,2,1,0:T(8,128)(2,1)S(1)}, bf16[2,16,8,256]{3,2,1,0:T(8,128)(2,1)}, u32[]{:S(2)}) copy-start(bf16[2,16,8,256]{3,2,1,0:T(8,128)(2,1)} %param.21) | copy-start | bytes 393220
  139.1 36.1 %copy-start.16 = (bf16[32]{0:T(256)(128)(2,1)S(1)}, bf16[32]{0:T(256)(128)(2,1)}, u32[]{:S(2)}) copy-start(bf16[32]{0:T(256)(128)(2,1)} %param.24) | copy-start | bytes 196
  139.1 36.0 %copy-start.14 = (s32[2,16,2]{1,2,0:T(2,128)S(1)}, s32[2,16,2]{1,2,0:T(2,128)}, u32[]{:S(2)}) copy-start(s32[2,16,2]{1,2,0:T(2,128)} %param.26) | copy-start | bytes 772
  139.1 76.0 %all-gather.11.cloned.1.call-start = ((), (), s32[]{:S(2)}) async-start(), calls=%async_computation.16 | async-start | bytes 2621440 | tf_op jit(solution)/shard_map/all_gather | solution.py:24
  172.3 178.0 %reduce-scatter.31.cloned.1.call-start = ((), (), s32[]{:S(2)}) async-start(), calls=%async_computation.26 | async-start | bytes 655360 | tf_op jit(solution)/shard_map/reduce_scatter | solution.py:54
  216.9 1.6 copy-start.5
  218.5 3.6 copy-start.15
  331.4 74.7 %copy-start.3 = (f32[128,8,32]{1,0,2:T(8,128)S(1)}, f32[128,8,32]{1,0,2:T(8,128)}, u32[]{:S(2)}) copy-start(f32[128,8,32]{1,0,2:T(8,128)} %get-tuple-element.40) | copy-start | bytes 393220
  331.4 42.6 %reduce-scatter.25.cloned.1.call-start = ((), (), s32[]{:S(2)}) async-start(), calls=%async_computation.23 | async-start | bytes 655360 | tf_op jit(solution)/shard_map/reduce_scatter | solution.py:54
  334.5 117.1 %copy-start.20 = (u32[128]{0:T(128)S(1)}, u32[128]{0:T(128)}, u32[]{:S(2)}) copy-start(u32[128]{0:T(128)} %constant.244) | copy-start | bytes 1540
  334.6 117.7 %copy-start.19 = (u32[128]{0:T(128)S(1)}, u32[128]{0:T(128)}, u32[]{:S(2)}) copy-start(u32[128]{0:T(128)} %constant.240) | copy-start | bytes 1540
  334.6 118.3 %copy-start.18 = (u32[128]{0:T(128)S(1)}, u32[128]{0:T(128)}, u32[]{:S(2)}) copy-start(u32[128]{0:T(128)} %constant.236) | copy-start | bytes 1540
  334.6 118.9 %copy-start.17 = (u32[128]{0:T(128)S(1)}, u32[128]{0:T(128)}, u32[]{:S(2)}) copy-start(u32[128]{0:T(128)} %constant.232) | copy-start | bytes 1540
  334.6 71.5 %reduce-scatter.13.cloned.1.call-start = ((), (), s32[]{:S(2)}) async-start(), calls=%async_computation.17 | async-start | bytes 2621440 | tf_op jit(solution)/shard_map/reduce_scatter | solution.py:54
  335.3 93.6 %reduce-scatter.33.cloned.1.call-start = ((), (), s32[]{:S(2)}) async-start(), calls=%async_computation.27 | async-start | bytes 163840 | tf_op jit(solution)/shard_map/reduce_scatter | solution.py:54
  350.4 101.2 %reduce-scatter.27.cloned.1.call-start = ((), (), s32[]{:S(2)}) async-start(), calls=%async_computation.24 | async-start | bytes 163840 | tf_op jit(solution)/shard_map/reduce_scatter | solution.py:54
  374.0 89.9 %reduce-scatter.15.cloned.1.call-start = ((), (), s32[]{:S(2)}) async-start(), calls=%async_computation.18 | async-start | bytes 786432 | tf_op jit(solution)/shard_map/reduce_scatter | solution.py:54
  406.1 72.1 %reduce-scatter.19.cloned.1.call-start = ((), (), s32[]{:S(2)}) async-start(), calls=%async_computation.20 | async-start | bytes 786432 | tf_op jit(solution)/shard_map/reduce_scatter | solution.py:54
  408.1 83.8 %reduce-scatter.35.cloned.1.call-start = ((), (), s32[]{:S(2)}) async-start(), calls=%async_computation.28 | async-start | bytes 49152 | tf_op jit(solution)/shard_map/reduce_scatter | solution.py:54
  429.0 87.6 %reduce-scatter.29.cloned.1.call-start = ((), (), s32[]{:S(2)}) async-start(), calls=%async_computation.25 | async-start | bytes 40960 | tf_op jit(solution)/shard_map/reduce_scatter | solution.py:54
  451.6 87.3 %reduce-scatter.17.cloned.1.call-start = ((), (), s32[]{:S(2)}) async-start(), calls=%async_computation.19 | async-start | bytes 81920 | tf_op jit(solution)/shard_map/reduce_scatter | solution.py:54
  465.7 137.7 %copy-start.1 = (bf16[12,8,64,256]{3,2,1,0:T(8,128)(2,1)S(1)}, bf16[12,8,64,256]{3,2,1,0:T(8,128)(2,1)}, u32[]{:S(2)}) copy-start(bf16[12,8,64,256]{3,2,1,0:T(8,128)(2,1)} %param.19) | copy-start | bytes 9437188
  465.7 96.0 %reduce-scatter.21.cloned.1.call-start = ((), (), s32[]{:S(2)}) async-start(), calls=%async_computation.21 | async-start | bytes 327680 | tf_op jit(solution)/shard_map/reduce_scatter | solution.py:54
  478.2 106.0 %reduce-scatter.23.cloned.1.call-start = ((), (), s32[]{:S(2)}) async-start(), calls=%async_computation.22 | async-start | bytes 81920 | tf_op jit(solution)/shard_map/reduce_scatter | solution.py:54
Sparse Core Ops, SparseCore 0:
  91.8 27.9 all-gather.4
  122.8 11.3 all-gather.6
  139.2 30.1 all-gather.8
  172.5 31.3 all-gather.10
  331.5 18.7 reduce-scatter.30
  352.6 21.3 reduce-scatter.24
  376.4 29.6 reduce-scatter.12
  408.4 20.4 reduce-scatter.32
  431.3 20.1 reduce-scatter.26
  453.7 10.1 reduce-scatter.14
  466.3 11.8 reduce-scatter.18
  480.4 11.5 reduce-scatter.34
  494.3 22.2 reduce-scatter.28
  518.7 20.0 reduce-scatter.16
  541.1 20.5 reduce-scatter.20
  563.9 20.3 reduce-scatter.22
where the time goes:
time: 611 us; the launch traced here: 610 us
  waiting for transfers between devices  268 us (44%)
  blocking collectives  224 us (37%)
  local copies, waits for them, and re-layouts  42 us (7%)
  other arithmetic  29.7 us (5%)
  matrix products  18.5 us (3%)
  between operations  14.7 us (2%)
  starting transfers between devices  12.4 us (2%)
    reduce_scatter x12, waiting for transfers between devices, own_block(): blocks = lax.psum_scatter(blocks, axes[k], scatter_dimension=0, tiled=True)  198 us
    all_gather x8, blocking collectives, joined_all(): pieces = jax.tree.map(lambda part: lax.all_gather(part, axis), array)  76.6 us
    all_gather x1, blocking collectives, body(): features = lax.all_gather(normed, SEQ_HEAD, axis=1, tiled=True)  60 us
    unnamed x4, blocking collectives  55.5 us
    all_to_all x1, waiting for transfers between devices, body(): lax.all_to_all(packed.reshape(device_count, capacity, PAGE, 2 * HD), SEQ_...  38 us
    psum x4, blocking collectives, over_axes(): array = lax.psum(array, axis)  32.2 us
    all_gather x4, waiting for transfers between devices, joined_all(): pieces = jax.tree.map(lambda part: lax.all_gather(part, axis), array)  31.1 us
  transfers between devices with their start and end apart: 17, of which 15 were waited for; matrix products, arithmetic and copies ran while one was open for 6% of the time, Pallas kernels for 0%

commit v1 on v0

--- a/solution.py
+++ b/solution.py
@@ -272,7 +272,7 @@
     inverse_rms = lax.rsqrt(squares / D + EPSILON)
     logits = routed * inverse_rms[:, None]
     normed = (middle * inverse_rms[:, None] * gain_row).astype(jnp.bfloat16)
-    features = lax.all_gather(normed, SEQ_HEAD, axis=1, tiled=True)
+    features = jnp.concatenate(lax.all_gather(normed, SEQ_HEAD), 1)
     mixture = gate_mix(logits, routes.reshape(row_count, TOPK))
     local_experts = w_gate.shape[0]
     local_mix = lax.dynamic_slice_in_dim(mixture, seq_pos * local_experts, local_experts, axis=1)

time: 611 us -> 613 us (level)
  no operation moved by 1% of the time
where the time goes in v1:
time: 613 us; the launch traced here: 611 us
  waiting for transfers between devices  268 us (44%)
  blocking collectives  224 us (37%)
  local copies, waits for them, and re-layouts  43.6 us (7%)
  other arithmetic  29.7 us (5%)
  matrix products  18.5 us (3%)
  between operations  14.7 us (2%)
  starting transfers between devices  12.4 us (2%)
    reduce_scatter x12, waiting for transfers between devices, own_block(): blocks = lax.psum_scatter(blocks, axes[k], scatter_dimension=0, tiled=True)  198 us
    all_gather x8, blocking collectives, joined_all(): pieces = jax.tree.map(lambda part: lax.all_gather(part, axis), array)  76.6 us
    all_gather x1, blocking collectives, body(): features = jnp.concatenate(lax.all_gather(normed, SEQ_HEAD), 1)  60 us
    unnamed x4, blocking collectives  55.5 us
    all_to_all x1, waiting for transfers between devices, body(): lax.all_to_all(packed.reshape(device_count, capacity, PAGE, 2 * HD), SEQ_...  38 us
    psum x4, blocking collectives, over_axes(): array = lax.psum(array, axis)  32.2 us
    all_gather x4, waiting for transfers between devices, joined_all(): pieces = jax.tree.map(lambda part: lax.all_gather(part, axis), array)  31.1 us
  transfers between devices with their start and end apart: 17, of which 15 were waited for; matrix products, arithmetic and copies ran while one was open for 6% of the time, Pallas kernels for 0%

profile of v1, /device:TPU:0, one launch (start us, length us, event | category | flops | bytes accessed | tf_op | source)
XLA Modules:
  0.0 611.5 jit_solution(472810552915857388)
XLA Ops:
  9.1 2.7 gather_fusion
  11.9 2.7 select_bitcast_fusion
  14.6 2.3 copy.241
  16.9 11.7 %all-to-all-start = ((bf16[128,1,64,256]{3,2,1,0:T(8,128)(2,1)}), bf16[128,1,64,256]{3,2,1,0:T(8,128)(2,1)}, u32[]{:S(2)}, u32[]{:S(2)}) async-start(bf16[128,1,64,256]{3,2,1,0:T(8,128)(2,1)} %bitcast.487), calls=%async_computation | async-start | bytes 8388608 | tf_op jit(solution)/shard_map/all_to_all | solution.py:205
  31.8 9.8 %fusion.130 = (s32[96]{0:T(128)S(1)}, s32[96]{0:T(128)S(1)}) fusion(s32[]{:T(128)} %bitcast.17, s32[]{:T(128)} %bitcast.18, s32[]{:T(128)} %bitcast.19, s32[]{:T(128)} %bitcast.20, s32[]{:T(128)} %bitcast.21, s32[]{:T(128)} %bitcast.22, s32[]{:T(128)} %bitcast.23, s32[]{:T(128)} %bitcast.24, s32[]{:T(128)} %bitcast.25, s32[]{:T(128)} %bitcast.26, ...), kind=kLoop, calls=%fused_computation.273 | loop fusion | flops 4032 | bytes 1600 | tf_op jit(solution)/shard_map/jit(_take)/select_n | solution.py:116
  41.7 38.0 %all-to-all-done = bf16[128,1,64,256]{3,2,1,0:T(8,128)(2,1)} async-done(((bf16[128,1,64,256]{3,2,1,0:T(8,128)(2,1)}), bf16[128,1,64,256]{3,2,1,0:T(8,128)(2,1)}, u32[]{:S(2)}, u32[]{:S(2)}) %all-to-all-start) | async-done | bytes 4194336 | tf_op jit(solution)/shard_map/all_to_all | solution.py:205
  79.7 3.0 gather_fusion.1
  88.4 2.0 fusion.8
  92.8 12.2 %all_gather.52 = f32[4,2,16,32]{3,2,1,0:T(8,128)S(1)} all-gather(f32[1,2,16,32]{3,2,1,0:T(8,128)S(1)} %copy.247), channel_id=1, replica_groups=mesh['seq_0'=4,'seq_1'=2,'head_0'=4,'head_1'=4] {'seq_0'}, dimensions={0}, use_global_device_ids=true | all-gather | bytes 20480 | tf_op jit(solution)/shard_map/all_gather | solution.py:24
  105.0 14.8 %all-gather.6.cloned.1.call-done = f32[4,2,16,32,128]{4,3,2,1,0:T(8,128)} async-done(((f32[1,2,16,32,128]{4,3,2,1,0:T(8,128)}), f32[4,2,16,32,128]{4,3,2,1,0:T(8,128)}) %all-gather.6.cloned.1.call-update) | async-done | bytes 2097168 | tf_op jit(solution)/shard_map/all_gather | solution.py:24
  119.8 2.9 fusion.45
  122.8 12.0 %all_gather.59 = f32[4,2,16,32]{3,2,1,0:T(8,128)S(1)} all-gather(f32[1,2,16,32]{3,2,1,0:T(8,128)S(1)} %copy.266), channel_id=1, replica_groups=mesh['seq_0'=4,'seq_1'=2,'head_0'=4,'head_1'=4] {'seq_0'}, dimensions={0}, use_global_device_ids=true | all-gather | bytes 20480 | tf_op jit(solution)/shard_map/all_gather | solution.py:24
  136.7 2.3 fusion.44
  141.0 12.1 %all_gather.56 = f32[4,2,16,32]{3,2,1,0:T(8,128)S(1)} all-gather(f32[1,2,16,32]{3,2,1,0:T(8,128)S(1)} %get-tuple-element.32), channel_id=1, replica_groups=mesh['seq_0'=4,'seq_1'=2,'head_0'=4,'head_1'=4] {'head_0'}, dimensions={0}, use_global_device_ids=true | all-gather | bytes 20480 | tf_op jit(solution)/shard_map/all_gather | solution.py:24
  153.1 16.3 %all-gather.10.cloned.1.call-done = f32[4,2,16,32,128]{4,3,2,1,0:T(8,128)} async-done(((f32[1,2,16,32,128]{4,3,2,1,0:T(8,128)}), f32[4,2,16,32,128]{4,3,2,1,0:T(8,128)}) %all-gather.10.cloned.1.call-update) | async-done | bytes 2097168 | tf_op jit(solution)/shard_map/all_gather | solution.py:24
  169.5 2.9 fusion.39
  172.5 2.4 fusion.152
  175.3 11.9 %all_gather.61 = f32[4,2,16,32]{3,2,1,0:T(8,128)S(1)} all-gather(f32[1,2,16,32]{3,2,1,0:T(8,128)S(1)} %get-tuple-element.31), channel_id=1, replica_groups=mesh['seq_0'=4,'seq_1'=2,'head_0'=4,'head_1'=4] {'head_0'}, dimensions={0}, use_global_device_ids=true | all-gather | bytes 20480 | tf_op jit(solution)/shard_map/all_gather | solution.py:24
  187.1 13.0 %all_gather.58 = f32[4,2,16,32]{3,2,1,0:T(8,128)S(1)} all-gather(f32[1,2,16,32]{3,2,1,0:T(8,128)S(1)} %get-tuple-element.30), channel_id=1, replica_groups=mesh['seq_0'=4,'seq_1'=2,'head_0'=4,'head_1'=4] {'head_1'}, dimensions={0}, use_global_device_ids=true | all-gather | bytes 20480 | tf_op jit(solution)/shard_map/all_gather | solution.py:24
  201.5 11.9 %all_gather.62 = f32[4,2,16,32]{3,2,1,0:T(8,128)S(1)} all-gather(f32[1,2,16,32]{3,2,1,0:T(8,128)S(1)} %get-tuple-element.29), channel_id=1, replica_groups=mesh['seq_0'=4,'seq_1'=2,'head_0'=4,'head_1'=4] {'head_1'}, dimensions={0}, use_global_device_ids=true | all-gather | bytes 20480 | tf_op jit(solution)/shard_map/all_gather | solution.py:24
  218.5 3.6 multiply_reduce_fusion
  222.3 10.7 %all-reduce.6 = (f32[32]{0:T(128)S(1)}, f32[32,8]{0,1:T(8,128)S(1)}) all-reduce(f32[32]{0:T(128)S(1)} %get-tuple-element.95, f32[32,8]{0,1:T(8,128)S(1)} %fusion.112), channel_id=1, replica_groups=mesh['seq_0'=4,'seq_1'=2,'head_0'=4,'head_1'=4] {'seq_0'}, use_global_device_ids=true, to_apply=%region_17.18 | all-reduce | flops 288 | bytes 2304 | tf_op jit(solution)/shard_map/psum | solution.py:33
  233.0 2.5 all-reduce.7
  235.5 8.7 %all-reduce.5 = (f32[32]{0:T(128)S(1)}, f32[32,8]{0,1:T(8,128)S(1)}) all-reduce(f32[32]{0:T(128)S(1)} %get-tuple-element.15, f32[32,8]{0,1:T(8,128)S(1)} %get-tuple-element.16), channel_id=1, replica_groups=mesh['seq_0'=4,'seq_1'=2,'head_0'=4,'head_1'=4] {'head_0'}, use_global_device_ids=true, to_apply=%region_19.20 | all-reduce | flops 288 | bytes 2304 | tf_op jit(solution)/shard_map/psum | solution.py:33
  244.3 10.3 %all-reduce.4 = (f32[32]{0:T(128)S(1)}, f32[32,8]{0,1:T(8,128)S(1)}) all-reduce(f32[32]{0:T(128)S(1)} %get-tuple-element.11, f32[32,8]{0,1:T(8,128)S(1)} %get-tuple-element.12), channel_id=1, replica_groups=mesh['seq_0'=4,'seq_1'=2,'head_0'=4,'head_1'=4] {'head_1'}, use_global_device_ids=true, to_apply=%region_20.21 | all-reduce | flops 288 | bytes 2304 | tf_op jit(solution)/shard_map/psum | solution.py:33
  254.7 60.0 %all-gather = bf16[4096,32]{1,0:T(8,128)(2,1)S(1)} all-gather(bf16[32,32]{1,0:T(8,128)(2,1)S(1)} %copy.275), channel_id=2, replica_groups=mesh['seq_0'=4,'seq_1'=2,'head_0'=4,'head_1'=4] {'seq_0','seq_1','head_0..., dimensions={0}, use_global_device_ids=true | all-gather | bytes 264192 | tf_op jit(solution)/shard_map/all_gather | solution.py:275
  316.3 3.0 fusion.14
  319.3 5.1 fusion
  325.1 4.9 fusion.144
  330.0 2.9 copy.281
  333.0 3.1 copy.280
  337.0 15.0 %reduce-scatter.31.cloned.1.call-done = f32[32,8,32]{2,1,0:T(8,128)} async-done(((f32[128,8,32]{2,1,0:T(8,128)}), f32[32,8,32]{2,1,0:T(8,128)}) %reduce-scatter.31.cloned.1.call-update) | async-done | bytes 32784 | tf_op jit(solution)/shard_map/reduce_scatter | solution.py:54
  352.0 23.5 %reduce-scatter.25.cloned.1.call-done = f32[32,8,32]{2,1,0:T(8,128)} async-done(((f32[128,8,32]{2,1,0:T(8,128)}), f32[32,8,32]{2,1,0:T(8,128)}) %reduce-scatter.25.cloned.1.call-update) | async-done | bytes 32784 | tf_op jit(solution)/shard_map/reduce_scatter | solution.py:54
  375.6 32.0 %reduce-scatter.13.cloned.1.call-done = f32[32,8,32]{1,0,2:T(8,128)} async-done(((f32[128,8,32]{1,0,2:T(8,128)}), f32[32,8,32]{1,0,2:T(8,128)}) %reduce-scatter.13.cloned.1.call-update) | async-done | bytes 32784 | tf_op jit(solution)/shard_map/reduce_scatter | solution.py:54
  409.7 20.8 %reduce-scatter.33.cloned.1.call-done = f32[8,8,32]{2,1,0:T(8,128)} async-done(((f32[32,8,32]{2,1,0:T(8,128)}), f32[8,8,32]{2,1,0:T(8,128)}) %reduce-scatter.33.cloned.1.call-update) | async-done | bytes 8208 | tf_op jit(solution)/shard_map/reduce_scatter | solution.py:54
  430.6 22.5 %reduce-scatter.27.cloned.1.call-done = f32[8,8,32]{2,1,0:T(8,128)} async-done(((f32[32,8,32]{2,1,0:T(8,128)}), f32[8,8,32]{2,1,0:T(8,128)}) %reduce-scatter.27.cloned.1.call-update) | async-done | bytes 8208 | tf_op jit(solution)/shard_map/reduce_scatter | solution.py:54
  455.7 9.8 %reduce-scatter.15.cloned.1.call-done = f32[16,8,32]{1,0,2:T(8,128)} async-done(((f32[32,8,32]{1,0,2:T(8,128)}), f32[16,8,32]{1,0,2:T(8,128)}) %reduce-scatter.15.cloned.1.call-update) | async-done | bytes 16400 | tf_op jit(solution)/shard_map/reduce_scatter | solution.py:54
  467.3 4.1 bitcast_select_fusion.1
  471.4 8.4 %reduce-scatter.19.cloned.1.call-done = f32[64,8,32]{2,1,0:T(8,128)} async-done(((f32[128,8,32]{2,1,0:T(8,128)}), f32[64,8,32]{2,1,0:T(8,128)}) %reduce-scatter.19.cloned.1.call-update) | async-done | bytes 65552 | tf_op jit(solution)/shard_map/reduce_scatter | solution.py:54
  479.9 13.6 %reduce-scatter.35.cloned.1.call-done = f32[4,8,32]{2,1,0:T(8,128)} async-done(((f32[8,8,32]{2,1,0:T(8,128)}), f32[4,8,32]{2,1,0:T(8,128)}) %reduce-scatter.35.cloned.1.call-update) | async-done | bytes 4112 | tf_op jit(solution)/shard_map/reduce_scatter | solution.py:54
  493.5 17.7 %all-reduce.3 = f32[4,8,32]{2,1,0:T(8,128)S(1)} all-reduce(f32[4,8,32]{2,1,0:T(8,128)} %reduce-scatter.35.cloned.1.call-done), channel_id=18, replica_groups=mesh['seq_0'=4,'seq_1'=2,'head_0'=4,'head_1'=4] {'head_0'}, use_global_device_ids=true, to_apply=%region_38.39.clone | all-reduce | flops 1024 | bytes 8192
  511.8 6.3 %reduce-scatter.29.cloned.1.call-done = f32[2,8,32]{2,1,0:T(8,128)} async-done(((f32[8,8,32]{2,1,0:T(8,128)}), f32[2,8,32]{2,1,0:T(8,128)}) %reduce-scatter.29.cloned.1.call-update) | async-done | bytes 2064 | tf_op jit(solution)/shard_map/reduce_scatter | solution.py:54
  518.1 2.6 all-reduce.2
  521.4 19.1 %reduce-scatter.17.cloned.1.call-done = f32[4,8,32]{2,1,0:T(8,128)} async-done(((f32[16,8,32]{2,1,0:T(8,128)}), f32[4,8,32]{2,1,0:T(8,128)}) %reduce-scatter.17.cloned.1.call-update) | async-done | bytes 4112 | tf_op jit(solution)/shard_map/reduce_scatter | solution.py:54
  540.4 17.5 %all-reduce = f32[4,8,32]{2,1,0:T(8,128)S(1)} all-reduce(f32[4,8,32]{2,1,0:T(8,128)} %reduce-scatter.17.cloned.1.call-done), channel_id=6, replica_groups=mesh['seq_0'=4,'seq_1'=2,'head_0'=4,'head_1'=4] {'head_1'}, use_global_device_ids=true, to_apply=%region_26.27.clone | all-reduce | flops 1024 | bytes 8192
  558.0 5.3 reduce-scatter.21.cloned.1.call-done
  563.9 22.0 %reduce-scatter.23.cloned.1.call-done = f32[4,8,32]{2,1,0:T(8,128)} async-done(((f32[16,8,32]{2,1,0:T(8,128)}), f32[4,8,32]{2,1,0:T(8,128)}) %reduce-scatter.23.cloned.1.call-update) | async-done | bytes 4112 | tf_op jit(solution)/shard_map/reduce_scatter | solution.py:54
  585.8 17.7 %all-reduce.1 = f32[4,8,32]{2,1,0:T(8,128)S(1)} all-reduce(f32[4,8,32]{2,1,0:T(8,128)} %reduce-scatter.23.cloned.1.call-done), channel_id=10, replica_groups=mesh['seq_0'=4,'seq_1'=2,'head_0'=4,'head_1'=4] {'seq_0'}, use_global_device_ids=true, to_apply=%region_30.31.clone | all-reduce | flops 1024 | bytes 8192
  (204 shorter events, 37.4 us)
Async XLA Ops:
  7.2 2.0 copy-start
  16.9 11.8 %copy-start.6 = (bf16[2,16,4096]{2,1,0:T(8,128)(2,1)S(1)}, bf16[2,16,4096]{2,1,0:T(8,128)(2,1)}, u32[]{:S(2)}) copy-start(bf16[2,16,4096]{2,1,0:T(8,128)(2,1)} %param.20) | copy-start | bytes 786436
  16.9 12.2 %copy-start.10 = (s32[1536]{0:T(1024)S(1)}, s32[1536]{0:T(1024)}, u32[]{:S(2)}) copy-start(s32[1536]{0:T(1024)} %param.18) | copy-start | bytes 18436
  16.9 12.2 %copy-start.12 = (s32[1536]{0:T(1024)S(1)}, s32[1536]{0:T(1024)}, u32[]{:S(2)}) copy-start(s32[1536]{0:T(1024)} %param.17) | copy-start | bytes 18436
  16.9 12.2 %copy-start.13 = (s32[1536]{0:T(1024)S(1)}, s32[1536]{0:T(1024)}, u32[]{:S(2)}) copy-start(s32[1536]{0:T(1024)} %param.16) | copy-start | bytes 18436
  16.9 14.2 %copy-start.9 = (s32[16]{0:T(128)S(1)}, s32[16]{0:T(128)}, u32[]{:S(2)}) copy-start(s32[16]{0:T(128)} %param.15) | copy-start | bytes 196
  16.9 62.8 %all-to-all-start = ((bf16[128,1,64,256]{3,2,1,0:T(8,128)(2,1)}), bf16[128,1,64,256]{3,2,1,0:T(8,128)(2,1)}, u32[]{:S(2)}, u32[]{:S(2)}) async-start(bf16[128,1,64,256]{3,2,1,0:T(8,128)(2,1)} %bitcast.487), calls=%async_computation | async-start | bytes 8388608 | tf_op jit(solution)/shard_map/all_to_all | solution.py:205
  28.6 91.2 %all-gather.6.cloned.1.call-start = ((), (), s32[]{:S(2)}) async-start(), calls=%async_computation.13 | async-start | bytes 2621440 | tf_op jit(solution)/shard_map/all_gather | solution.py:24
  82.7 1.7 copy-start.2
  82.7 3.3 copy-start.7
  84.3 1.7 copy-start.4
  91.7 45.0 %all-gather.8.cloned.1.call-start = ((), (), s32[]{:S(2)}) async-start(), calls=%async_computation.14 | async-start | bytes 1572864 | tf_op jit(solution)/shard_map/all_gather | solution.py:24
  122.7 49.7 %copy-start.11 = (bf16[2,16,32]{2,1,0:T(8,128)(2,1)S(1)}, bf16[2,16,32]{2,1,0:T(8,128)(2,1)}, u32[]{:S(2)}) copy-start(bf16[2,16,32]{2,1,0:T(8,128)(2,1)} %param.22) | copy-start | bytes 6148
  122.7 46.8 %all-gather.10.cloned.1.call-start = ((), (), s32[]{:S(2)}) async-start(), calls=%async_computation.15 | async-start | bytes 2621440 | tf_op jit(solution)/shard_map/all_gather | solution.py:24
  122.8 49.7 %copy-start.8 = (bf16[2,16,8,256]{3,2,1,0:T(8,128)(2,1)S(1)}, bf16[2,16,8,256]{3,2,1,0:T(8,128)(2,1)}, u32[]{:S(2)}) copy-start(bf16[2,16,8,256]{3,2,1,0:T(8,128)(2,1)} %param.21) | copy-start | bytes 393220
  139.1 36.1 %copy-start.16 = (bf16[32]{0:T(256)(128)(2,1)S(1)}, bf16[32]{0:T(256)(128)(2,1)}, u32[]{:S(2)}) copy-start(bf16[32]{0:T(256)(128)(2,1)} %param.24) | copy-start | bytes 196
  139.1 36.0 %copy-start.14 = (s32[2,16,2]{1,2,0:T(2,128)S(1)}, s32[2,16,2]{1,2,0:T(2,128)}, u32[]{:S(2)}) copy-start(s32[2,16,2]{1,2,0:T(2,128)} %param.26) | copy-start | bytes 772
  139.1 76.0 %all-gather.12.cloned.1.call-start = ((), (), s32[]{:S(2)}) async-start(), calls=%async_computation.16 | async-start | bytes 2621440 | tf_op jit(solution)/shard_map/all_gather | solution.py:24
  172.3 179.6 %reduce-scatter.31.cloned.1.call-start = ((), (), s32[]{:S(2)}) async-start(), calls=%async_computation.26 | async-start | bytes 655360 | tf_op jit(solution)/shard_map/reduce_scatter | solution.py:54
  216.9 1.6 copy-start.5
  218.5 3.6 copy-start.15
  333.0 74.7 %copy-start.3 = (f32[128,8,32]{1,0,2:T(8,128)S(1)}, f32[128,8,32]{1,0,2:T(8,128)}, u32[]{:S(2)}) copy-start(f32[128,8,32]{1,0,2:T(8,128)} %get-tuple-element.40) | copy-start | bytes 393220
  333.0 42.6 %reduce-scatter.25.cloned.1.call-start = ((), (), s32[]{:S(2)}) async-start(), calls=%async_computation.23 | async-start | bytes 655360 | tf_op jit(solution)/shard_map/reduce_scatter | solution.py:54
  336.1 117.1 %copy-start.20 = (u32[128]{0:T(128)S(1)}, u32[128]{0:T(128)}, u32[]{:S(2)}) copy-start(u32[128]{0:T(128)} %constant.244) | copy-start | bytes 1540
  336.1 117.7 %copy-start.19 = (u32[128]{0:T(128)S(1)}, u32[128]{0:T(128)}, u32[]{:S(2)}) copy-start(u32[128]{0:T(128)} %constant.240) | copy-start | bytes 1540
  336.1 118.3 %copy-start.18 = (u32[128]{0:T(128)S(1)}, u32[128]{0:T(128)}, u32[]{:S(2)}) copy-start(u32[128]{0:T(128)} %constant.236) | copy-start | bytes 1540
  336.2 118.9 %copy-start.17 = (u32[128]{0:T(128)S(1)}, u32[128]{0:T(128)}, u32[]{:S(2)}) copy-start(u32[128]{0:T(128)} %constant.232) | copy-start | bytes 1540
  336.2 71.5 %reduce-scatter.13.cloned.1.call-start = ((), (), s32[]{:S(2)}) async-start(), calls=%async_computation.17 | async-start | bytes 2621440 | tf_op jit(solution)/shard_map/reduce_scatter | solution.py:54
  336.9 93.6 %reduce-scatter.33.cloned.1.call-start = ((), (), s32[]{:S(2)}) async-start(), calls=%async_computation.27 | async-start | bytes 163840 | tf_op jit(solution)/shard_map/reduce_scatter | solution.py:54
  352.0 101.1 %reduce-scatter.27.cloned.1.call-start = ((), (), s32[]{:S(2)}) async-start(), calls=%async_computation.24 | async-start | bytes 163840 | tf_op jit(solution)/shard_map/reduce_scatter | solution.py:54
  375.6 89.9 %reduce-scatter.15.cloned.1.call-start = ((), (), s32[]{:S(2)}) async-start(), calls=%async_computation.18 | async-start | bytes 786432 | tf_op jit(solution)/shard_map/reduce_scatter | solution.py:54
  407.7 72.1 %reduce-scatter.19.cloned.1.call-start = ((), (), s32[]{:S(2)}) async-start(), calls=%async_computation.20 | async-start | bytes 786432 | tf_op jit(solution)/shard_map/reduce_scatter | solution.py:54
  409.7 83.8 %reduce-scatter.35.cloned.1.call-start = ((), (), s32[]{:S(2)}) async-start(), calls=%async_computation.28 | async-start | bytes 49152 | tf_op jit(solution)/shard_map/reduce_scatter | solution.py:54
  430.5 87.6 %reduce-scatter.29.cloned.1.call-start = ((), (), s32[]{:S(2)}) async-start(), calls=%async_computation.25 | async-start | bytes 40960 | tf_op jit(solution)/shard_map/reduce_scatter | solution.py:54
  453.1 87.3 %reduce-scatter.17.cloned.1.call-start = ((), (), s32[]{:S(2)}) async-start(), calls=%async_computation.19 | async-start | bytes 81920 | tf_op jit(solution)/shard_map/reduce_scatter | solution.py:54
  467.2 137.7 %copy-start.1 = (bf16[12,8,64,256]{3,2,1,0:T(8,128)(2,1)S(1)}, bf16[12,8,64,256]{3,2,1,0:T(8,128)(2,1)}, u32[]{:S(2)}) copy-start(bf16[12,8,64,256]{3,2,1,0:T(8,128)(2,1)} %param.19) | copy-start | bytes 9437188
  467.3 96.0 %reduce-scatter.21.cloned.1.call-start = ((), (), s32[]{:S(2)}) async-start(), calls=%async_computation.21 | async-start | bytes 327680 | tf_op jit(solution)/shard_map/reduce_scatter | solution.py:54
  479.8 106.0 %reduce-scatter.23.cloned.1.call-start = ((), (), s32[]{:S(2)}) async-start(), calls=%async_computation.22 | async-start | bytes 81920 | tf_op jit(solution)/shard_map/reduce_scatter | solution.py:54
Sparse Core Ops, SparseCore 0:
  91.8 27.9 all-gather.5
  122.8 11.3 all-gather.7
  139.2 30.1 all-gather.9
  172.5 31.3 all-gather.11
  333.1 18.8 reduce-scatter.30
  354.2 21.3 reduce-scatter.24
  378.0 29.6 reduce-scatter.12
  410.0 20.4 reduce-scatter.32
  432.9 20.1 reduce-scatter.26
  455.3 10.1 reduce-scatter.14
  467.9 11.8 reduce-scatter.18
  481.9 11.5 reduce-scatter.34
  495.9 22.2 reduce-scatter.28
  520.3 20.0 reduce-scatter.16
  542.6 20.5 reduce-scatter.20
  565.5 20.3 reduce-scatter.22
